TPU v7x, 32 devices: a whole 2x2x4 slice. The times are simulated.
32 devices in a mesh: layer: 2 (over x), blk: 16 (over z, y, core).
Axes of the slice: x: 2, y: 2, z: 4, core: 2. Of those that a mesh axis runs over, the one named last changes fastest.
Arguments:
- points: bfloat16 [12288, 256], P('blk'), may hold values from -8.4 to 8.4
- labels: int32 [12288], P('blk'), may hold values from 0 to 255, as said below
Outputs:
- distance: float32 [12288, 256], P('blk')
Inputs may be any that keep to these rules, and one draw needn't show every extreme that they name: `labels`: every cluster is named by at least one point.
All inputs are finite; a program needn't handle non-finite values.
Results may differ from a plain program's by a relative error of at most 0.00034.
Values may be sent and summed in bfloat16 or wider, within the bound.
A program may use at most 64 MiB of HBM per device.

v0:
```python
import jax
import jax.numpy as jnp
from jax import lax
from jax.sharding import PartitionSpec as P

K = 256


def as_sent(x):
    return jax.tree.map(lambda a: a.astype(jnp.bfloat16) if a.dtype == jnp.float32 else a, x)


def from_behind(x, axis, by):
    devices = lax.axis_size(axis)
    return lax.ppermute(x, axis, [(i, (i + by) % devices) for i in range(devices)])


def choose_where(chosen, shifted, carried):
    return tuple(
        (jnp.where(chosen, new_part, old_part) for new_part, old_part in zip(shifted, carried))
    )


def shards(points, labels):
    feature_width = points.shape[1]
    own_rows = points.shape[0]
    layers = lax.axis_size("layer")
    blocks = lax.axis_size("blk")
    visit_count = blocks // layers
    half_steps = visit_count // 2
    layer_idx = lax.axis_index("layer")
    offset_bits = (layers - 1).bit_length()
    own_sq = jnp.sum(jnp.square(points.astype(jnp.float32)), axis=1)
    cluster_ids = jnp.arange(K, dtype=jnp.float32)
    tagged = labels.astype(jnp.bfloat16)

    def accumulate(partial_value, visiting, block_tags):
        visit_sq = jnp.sum(jnp.square(visiting.astype(jnp.float32)), axis=1)
        gram_block = lax.dot_general(
            points, visiting, (((1,), (1,)), ((), ())), preferred_element_type=jnp.float32
        )
        kernel = jnp.exp(
            -(own_sq[:, None] + visit_sq[None, :] - 2.0 * gram_block) / feature_width
        ).astype(jnp.bfloat16)
        onehot = (block_tags.astype(jnp.float32)[:, None] == cluster_ids[None, :]).astype(
            jnp.bfloat16
        )
        return partial_value + jnp.dot(kernel, onehot, preferred_element_type=jnp.float32)

    initial = jnp.zeros((own_rows, K), jnp.float32)
    carried = (points, tagged)
    for bit_pos in range(offset_bits):
        shifted = jax.tree.map(
            lambda part, own: part.astype(own.dtype),
            from_behind(as_sent(carried), "blk", visit_count << bit_pos),
            carried,
        )
        carried = choose_where(layer_idx >> bit_pos & 1 == 1, shifted, carried)
    climbing = jax.tree.map(
        lambda part, own: part.astype(own.dtype),
        from_behind(as_sent(carried), "blk", half_steps),
        carried,
    )
    falling = jax.tree.map(
        lambda part, own: part.astype(own.dtype),
        from_behind(as_sent(carried), "blk", half_steps - 1),
        carried,
    )
    partial_value = accumulate(
        accumulate(initial, climbing[0], climbing[1]), falling[0], falling[1]
    )

    def split_turn(turn_index, loop_state):
        partial_now, climb_pts, climb_tags, fall_pts, fall_tags = loop_state
        climb_pts, climb_tags = from_behind((climb_pts, climb_tags), "blk", 1)
        fall_pts, fall_tags = from_behind((fall_pts, fall_tags), "blk", -1)
        partial_now = accumulate(partial_now, climb_pts, climb_tags)
        partial_now = accumulate(partial_now, fall_pts, fall_tags)
        return (partial_now, climb_pts, climb_tags, fall_pts, fall_tags)

    partial_value = lax.fori_loop(
        0,
        half_steps - 1,
        split_turn,
        (partial_value, climbing[0], climbing[1], falling[0], falling[1]),
    )[0]
    row_sums = lax.psum(partial_value, "layer")
    member_f = (labels[:, None] == jnp.arange(K, dtype=jnp.int32)[None, :]).astype(jnp.float32)
    within, counts = lax.psum(
        (jnp.sum(member_f * row_sums, axis=0), jnp.sum(member_f, axis=0)), "blk"
    )
    distance = 1.0 - 2.0 * row_sums / counts[None, :] + within[None, :] / (counts * counts)[None, :]
    return distance


def solution(mesh):
    in_specs = (P("blk", None), P("blk"))
    out_specs = P("blk", None)
    return jax.shard_map(shards, mesh=mesh, in_specs=in_specs, out_specs=out_specs, check_vma=False)
```

profile of v0, /device:TPU:0, one launch (start us, length us, event | category | flops | bytes accessed | tf_op | source)
XLA Modules:
  0.0 178.2 jit_solution(9994201577379634457)
XLA Ops:
  6.5 4.1 %collective-permute-start.4 = (bf16[768,256]{1,0:T(8,128)(2,1)}, bf16[768,256]{1,0:T(8,128)(2,1)S(1)}, u32[]{:S(2)}, u32[]{:S(2)}) collective-permute-start(bf16[768,256]{1,0:T(8,128)(2,1)} %param.4), channel_id=1, source_target_pairs={{0,8},{1,9},{2,10},{3,11},{4,12},{5,13},{6,14},{7,15},{8,0},{9,1},... | collective-permute-start | bytes 1179656 | tf_op jit(solution)/shard_map/ppermute | solution.py:15
  10.6 17.8 %collective-permute-done.4 = bf16[768,256]{1,0:T(8,128)(2,1)S(1)} collective-permute-done((bf16[768,256]{1,0:T(8,128)(2,1)}, bf16[768,256]{1,0:T(8,128)(2,1)S(1)}, u32[]{:S(2)}, u32[]{:S(2)}) %collective-permute-start.4) | collective-permute-done | bytes 393248 | tf_op jit(solution)/shard_map/ppermute | solution.py:15
  29.7 5.0 %collective-permute-start.5 = (bf16[768,256]{1,0:T(8,128)(2,1)S(1)}, bf16[768,256]{1,0:T(8,128)(2,1)S(1)}, u32[]{:S(2)}, u32[]{:S(2)}) collective-permute-start(bf16[768,256]{1,0:T(8,128)(2,1)S(1)} %broadcast_select_fusion), channel_id=1, source_target_pairs={{0,4},{1,5},{2,6},{3,7},{4,8},{5,9},{6,10},{7,11},{8,12},{9,13},{1... | collective-permute-start | bytes 1179656 | tf_op jit(solution)/shard_map/ppermute | solution.py:15
  34.7 5.6 %collective-permute-start.9 = (bf16[768]{0:T(1024)(128)(2,1)S(1)}, bf16[768]{0:T(1024)(128)(2,1)S(1)}, u32[]{:S(2)}, u32[]{:S(2)}) collective-permute-start(bf16[768]{0:T(1024)(128)(2,1)S(1)} %broadcast_select_fusion.1), channel_id=1, source_target_pairs={{0,3},{1,4},{2,5},{3,6},{4,7},{5,8},{6,9},{7,10},{8,11},{9,12},{10... | collective-permute-start | bytes 4616 | tf_op jit(solution)/shard_map/ppermute | solution.py:15
  40.4 3.7 %collective-permute-start.7 = (bf16[768]{0:T(1024)(128)(2,1)S(1)}, bf16[768]{0:T(1024)(128)(2,1)S(1)}, u32[]{:S(2)}, u32[]{:S(2)}) collective-permute-start(bf16[768]{0:T(1024)(128)(2,1)S(1)} %broadcast_select_fusion.1), channel_id=1, source_target_pairs={{0,4},{1,5},{2,6},{3,7},{4,8},{5,9},{6,10},{7,11},{8,12},{9,13},{1... | collective-permute-start | bytes 4616 | tf_op jit(solution)/shard_map/ppermute | solution.py:15
  44.3 2.8 %collective-permute-done.9 = bf16[768]{0:T(1024)(128)(2,1)S(1)} collective-permute-done((bf16[768]{0:T(1024)(128)(2,1)S(1)}, bf16[768]{0:T(1024)(128)(2,1)S(1)}, u32[]{:S(2)}, u32[]{:S(2)}) %collective-permute-start.9) | collective-permute-done | bytes 1568 | tf_op jit(solution)/shard_map/ppermute | solution.py:15
  49.3 50.8 %while.20 = (s32[]{:T(128)}, f32[768,256]{1,0:T(8,128)S(1)}, bf16[768,256]{1,0:T(8,128)(2,1)S(1)}, bf16[768]{0:T(1024)(128)(2,1)S(1)}, bf16[768,256]{1,0:T(8,128...) while((s32[]{:T(128)}, f32[768,256]{1,0:T(8,128)S(1)}, ...), condition=%wide.region_6.7_spmd.clone.clone, body=%wide.region_3.6_spmd.clone.clone.sunk | while | flops 1217003520 | bytes 10276093 | solution.py:81
  49.4 6.5 %collective-permute-start = (bf16[768,256]{1,0:T(8,128)(2,1)S(1)}, bf16[768,256]{1,0:T(8,128)(2,1)S(1)}, u32[]{:S(2)}, u32[]{:S(2)}) collective-permute-start(bf16[768,256]{1,0:T(8,128)(2,1)S(1)} %get-tuple-element.178), channel_id=1, source_target_pairs={{0,15},{1,0},{2,1},{3,2},{4,3},{5,4},{6,5},{7,6},{8,7},{9,8},{10,9... | collective-permute-start | bytes 1179656 | tf_op jit(solution)/shard_map/while/body/eval_jaxpr/ppermute | solution.py:15
  55.8 4.4 %collective-permute-start.1 = (bf16[768]{0:T(1024)(128)(2,1)S(1)}, bf16[768]{0:T(1024)(128)(2,1)S(1)}, u32[]{:S(2)}, u32[]{:S(2)}) collective-permute-start(bf16[768]{0:T(1024)(128)(2,1)S(1)} %get-tuple-element.179), channel_id=1, source_target_pairs={{0,15},{1,0},{2,1},{3,2},{4,3},{5,4},{6,5},{7,6},{8,7},{9,8},{10,9... | collective-permute-start | bytes 4616 | tf_op jit(solution)/shard_map/while/body/eval_jaxpr/ppermute | solution.py:15
  61.6 4.4 %collective-permute-done.3 = bf16[768]{0:T(1024)(128)(2,1)S(1)} collective-permute-done((bf16[768]{0:T(1024)(128)(2,1)S(1)}, bf16[768]{0:T(1024)(128)(2,1)S(1)}, u32[]{:S(2)}, u32[]{:S(2)}) %collective-permute-start.3) | collective-permute-done | bytes 1568 | tf_op jit(solution)/shard_map/while/body/eval_jaxpr/ppermute | solution.py:15
  66.5 1.8 %fusion.63 = f32[768,256]{1,0:T(8,128)} fusion(bf16[768,256]{1,0:T(8,128)(2,1)S(1)} %get-tuple-element.190, bf16[768,256]{1,0:T(8,128)(2,1)S(1)} %collective-permute-done, f32[768]{0:T(1024)S(1)} %multiply_reduce_fusion.7, f32[768]{0:T(1024)S(1)} %get-tuple-element.189, f32[768]{0:T(1024)S(1)} %convert_element_type.105), kind=kOutput, calls=%fused_computation.4.clone.1 | convolution fusion | flops 607715328 | bytes 1582080 | tf_op jit(solution)/shard_map/while/body/eval_jaxpr/dot_general | solution.py:48
  68.3 2.2 %fusion.64 = f32[768,256]{1,0:T(8,128)S(1)} fusion(f32[768,256]{1,0:T(8,128)} %fusion.63, f32[768,256]{1,0:T(8,128)S(1)} %get-tuple-element.175, bf16[768,256]{1,0:T(8,128)(2,1)S(1)} %get-tuple-element.190, bf16[768,256]{1,0:T(8,128)(2,1)S(1)} %collective-permute-done.2, f32[768]{0:T(1024)S(1)} %multiply_reduce_fusion.8, ...), kind=kOutput, calls=%fused_computation.6.clone.1 | convolution fusion | flops 608108544 | bytes 3154944 | tf_op jit(solution)/shard_map/while/body/eval_jaxpr/dot_general | solution.py:48
  71.1 4.0 %collective-permute-start.1 = (bf16[768]{0:T(1024)(128)(2,1)S(1)}, bf16[768]{0:T(1024)(128)(2,1)S(1)}, u32[]{:S(2)}, u32[]{:S(2)}) collective-permute-start(bf16[768]{0:T(1024)(128)(2,1)S(1)} %get-tuple-element.179), channel_id=1, source_target_pairs={{0,15},{1,0},{2,1},{3,2},{4,3},{5,4},{6,5},{7,6},{8,7},{9,8},{10,9... | collective-permute-start | bytes 4616 | tf_op jit(solution)/shard_map/while/body/eval_jaxpr/ppermute | solution.py:15
  76.4 4.4 %collective-permute-done.3 = bf16[768]{0:T(1024)(128)(2,1)S(1)} collective-permute-done((bf16[768]{0:T(1024)(128)(2,1)S(1)}, bf16[768]{0:T(1024)(128)(2,1)S(1)}, u32[]{:S(2)}, u32[]{:S(2)}) %collective-permute-start.3) | collective-permute-done | bytes 1568 | tf_op jit(solution)/shard_map/while/body/eval_jaxpr/ppermute | solution.py:15
  81.3 1.8 %fusion.63 = f32[768,256]{1,0:T(8,128)} fusion(bf16[768,256]{1,0:T(8,128)(2,1)S(1)} %get-tuple-element.190, bf16[768,256]{1,0:T(8,128)(2,1)S(1)} %collective-permute-done, f32[768]{0:T(1024)S(1)} %multiply_reduce_fusion.7, f32[768]{0:T(1024)S(1)} %get-tuple-element.189, f32[768]{0:T(1024)S(1)} %convert_element_type.105), kind=kOutput, calls=%fused_computation.4.clone.1 | convolution fusion | flops 607715328 | bytes 1582080 | tf_op jit(solution)/shard_map/while/body/eval_jaxpr/dot_general | solution.py:48
  83.1 2.2 %fusion.64 = f32[768,256]{1,0:T(8,128)S(1)} fusion(f32[768,256]{1,0:T(8,128)} %fusion.63, f32[768,256]{1,0:T(8,128)S(1)} %get-tuple-element.175, bf16[768,256]{1,0:T(8,128)(2,1)S(1)} %get-tuple-element.190, bf16[768,256]{1,0:T(8,128)(2,1)S(1)} %collective-permute-done.2, f32[768]{0:T(1024)S(1)} %multiply_reduce_fusion.8, ...), kind=kOutput, calls=%fused_computation.6.clone.1 | convolution fusion | flops 608108544 | bytes 3154944 | tf_op jit(solution)/shard_map/while/body/eval_jaxpr/dot_general | solution.py:48
  85.4 1.4 collective-permute-start.2
  86.9 3.0 %collective-permute-start.1 = (bf16[768]{0:T(1024)(128)(2,1)S(1)}, bf16[768]{0:T(1024)(128)(2,1)S(1)}, u32[]{:S(2)}, u32[]{:S(2)}) collective-permute-start(bf16[768]{0:T(1024)(128)(2,1)S(1)} %get-tuple-element.179), channel_id=1, source_target_pairs={{0,15},{1,0},{2,1},{3,2},{4,3},{5,4},{6,5},{7,6},{8,7},{9,8},{10,9... | collective-permute-start | bytes 4616 | tf_op jit(solution)/shard_map/while/body/eval_jaxpr/ppermute | solution.py:15
  91.2 4.4 %collective-permute-done.3 = bf16[768]{0:T(1024)(128)(2,1)S(1)} collective-permute-done((bf16[768]{0:T(1024)(128)(2,1)S(1)}, bf16[768]{0:T(1024)(128)(2,1)S(1)}, u32[]{:S(2)}, u32[]{:S(2)}) %collective-permute-start.3) | collective-permute-done | bytes 1568 | tf_op jit(solution)/shard_map/while/body/eval_jaxpr/ppermute | solution.py:15
  96.1 1.8 %fusion.63 = f32[768,256]{1,0:T(8,128)} fusion(bf16[768,256]{1,0:T(8,128)(2,1)S(1)} %get-tuple-element.190, bf16[768,256]{1,0:T(8,128)(2,1)S(1)} %collective-permute-done, f32[768]{0:T(1024)S(1)} %multiply_reduce_fusion.7, f32[768]{0:T(1024)S(1)} %get-tuple-element.189, f32[768]{0:T(1024)S(1)} %convert_element_type.105), kind=kOutput, calls=%fused_computation.4.clone.1 | convolution fusion | flops 607715328 | bytes 1582080 | tf_op jit(solution)/shard_map/while/body/eval_jaxpr/dot_general | solution.py:48
  97.9 2.2 %fusion.64 = f32[768,256]{1,0:T(8,128)S(1)} fusion(f32[768,256]{1,0:T(8,128)} %fusion.63, f32[768,256]{1,0:T(8,128)S(1)} %get-tuple-element.175, bf16[768,256]{1,0:T(8,128)(2,1)S(1)} %get-tuple-element.190, bf16[768,256]{1,0:T(8,128)(2,1)S(1)} %collective-permute-done.2, f32[768]{0:T(1024)S(1)} %multiply_reduce_fusion.8, ...), kind=kOutput, calls=%fused_computation.6.clone.1 | convolution fusion | flops 608108544 | bytes 3154944 | tf_op jit(solution)/shard_map/while/body/eval_jaxpr/dot_general | solution.py:48
  101.1 34.8 %all-reduce.3.cloned.1.call-done = f32[768,256]{1,0:T(8,128)} async-done(((f32[768,256]{1,0:T(8,128)}), f32[768,256]{1,0:T(8,128)}) %all-reduce.3.cloned.1.call-update) | async-done | bytes 786448 | tf_op jit(solution)/shard_map/psum | solution.py:87
  135.9 1.4 convert_reduce_fusion
  137.3 33.0 %all-reduce = (f32[256]{0:T(256)S(1)}, f32[256]{0:T(256)S(1)}) all-reduce(f32[256]{0:T(256)S(1)} %get-tuple-element.97, f32[256]{0:T(256)S(1)} %get-tuple-element.96), channel_id=1, replica_groups=mesh['layer'=2,'blk'=16] {'blk'}, use_global_device_ids=true, to_apply=%region_11.12 | all-reduce | flops 512 | bytes 4096 | tf_op jit(solution)/shard_map/psum | solution.py:89
  (68 shorter events, 11.4 us)
Async XLA Ops:
  6.5 37.6 %copy-start.1 = (bf16[768,256]{1,0:T(8,128)(2,1)S(1)}, bf16[768,256]{1,0:T(8,128)(2,1)}, u32[]{:S(2)}) copy-start(bf16[768,256]{1,0:T(8,128)(2,1)} %param.4) | copy-start | bytes 1179652
  6.5 23.1 %copy-start.3 = (s32[768]{0:T(1024)S(1)}, s32[768]{0:T(1024)}, u32[]{:S(2)}) copy-start(s32[768]{0:T(1024)} %param.5) | copy-start | bytes 9220
  6.5 129.4 %all-reduce.3.cloned.1.call-start = ((), (), s32[]{:S(2)}) async-start(), calls=%async_computation | async-start | bytes 1572864 | tf_op jit(solution)/shard_map/psum | solution.py:87
  6.5 21.9 %collective-permute-start.4 = (bf16[768,256]{1,0:T(8,128)(2,1)}, bf16[768,256]{1,0:T(8,128)(2,1)S(1)}, u32[]{:S(2)}, u32[]{:S(2)}) collective-permute-start(bf16[768,256]{1,0:T(8,128)(2,1)} %param.4), channel_id=1, source_target_pairs={{0,8},{1,9},{2,10},{3,11},{4,12},{5,13},{6,14},{7,15},{8,0},{9,1},... | collective-permute-start | bytes 1179656 | tf_op jit(solution)/shard_map/ppermute | solution.py:15
  29.5 17.6 %collective-permute-start.8 = (bf16[768,256]{1,0:T(8,128)(2,1)S(1)}, bf16[768,256]{1,0:T(8,128)(2,1)S(1)}, u32[]{:S(2)}, u32[]{:S(2)}) collective-permute-start(bf16[768,256]{1,0:T(8,128)(2,1)S(1)} %broadcast_select_fusion), channel_id=1, source_target_pairs={{0,3},{1,4},{2,5},{3,6},{4,7},{5,8},{6,9},{7,10},{8,11},{9,12},{10... | collective-permute-start | bytes 1179656 | tf_op jit(solution)/shard_map/ppermute | solution.py:15
  29.7 5.1 %collective-permute-start.6 = (bf16[768]{0:T(1024)(128)(2,1)S(1)}, bf16[768]{0:T(1024)(128)(2,1)S(1)}, u32[]{:S(2)}, u32[]{:S(2)}) collective-permute-start(bf16[768]{0:T(1024)(128)(2,1)S(1)} %convert_element_type.52), channel_id=1, source_target_pairs={{0,8},{1,9},{2,10},{3,11},{4,12},{5,13},{6,14},{7,15},{8,0},{9,1},... | collective-permute-start | bytes 4616 | tf_op jit(solution)/shard_map/ppermute | solution.py:15
  29.7 17.6 %collective-permute-start.5 = (bf16[768,256]{1,0:T(8,128)(2,1)S(1)}, bf16[768,256]{1,0:T(8,128)(2,1)S(1)}, u32[]{:S(2)}, u32[]{:S(2)}) collective-permute-start(bf16[768,256]{1,0:T(8,128)(2,1)S(1)} %broadcast_select_fusion), channel_id=1, source_target_pairs={{0,4},{1,5},{2,6},{3,7},{4,8},{5,9},{6,10},{7,11},{8,12},{9,13},{1... | collective-permute-start | bytes 1179656 | tf_op jit(solution)/shard_map/ppermute | solution.py:15
  34.7 12.3 %collective-permute-start.9 = (bf16[768]{0:T(1024)(128)(2,1)S(1)}, bf16[768]{0:T(1024)(128)(2,1)S(1)}, u32[]{:S(2)}, u32[]{:S(2)}) collective-permute-start(bf16[768]{0:T(1024)(128)(2,1)S(1)} %broadcast_select_fusion.1), channel_id=1, source_target_pairs={{0,3},{1,4},{2,5},{3,6},{4,7},{5,8},{6,9},{7,10},{8,11},{9,12},{10... | collective-permute-start | bytes 4616 | tf_op jit(solution)/shard_map/ppermute | solution.py:15
  40.4 6.7 %collective-permute-start.7 = (bf16[768]{0:T(1024)(128)(2,1)S(1)}, bf16[768]{0:T(1024)(128)(2,1)S(1)}, u32[]{:S(2)}, u32[]{:S(2)}) collective-permute-start(bf16[768]{0:T(1024)(128)(2,1)S(1)} %broadcast_select_fusion.1), channel_id=1, source_target_pairs={{0,4},{1,5},{2,6},{3,7},{4,8},{5,9},{6,10},{7,11},{8,12},{9,13},{1... | collective-permute-start | bytes 4616 | tf_op jit(solution)/shard_map/ppermute | solution.py:15
  49.4 16.6 %collective-permute-start = (bf16[768,256]{1,0:T(8,128)(2,1)S(1)}, bf16[768,256]{1,0:T(8,128)(2,1)S(1)}, u32[]{:S(2)}, u32[]{:S(2)}) collective-permute-start(bf16[768,256]{1,0:T(8,128)(2,1)S(1)} %get-tuple-element.178), channel_id=1, source_target_pairs={{0,15},{1,0},{2,1},{3,2},{4,3},{5,4},{6,5},{7,6},{8,7},{9,8},{10,9... | collective-permute-start | bytes 1179656 | tf_op jit(solution)/shard_map/while/body/eval_jaxpr/ppermute | solution.py:15
  55.8 10.4 %collective-permute-start.2 = (bf16[768,256]{1,0:T(8,128)(2,1)S(1)}, bf16[768,256]{1,0:T(8,128)(2,1)S(1)}, u32[]{:S(2)}, u32[]{:S(2)}) collective-permute-start(bf16[768,256]{1,0:T(8,128)(2,1)S(1)} %get-tuple-element.176), channel_id=1, source_target_pairs={{0,1},{1,2},{2,3},{3,4},{4,5},{5,6},{6,7},{7,8},{8,9},{9,10},{10,1... | collective-permute-start | bytes 1179656 | tf_op jit(solution)/shard_map/while/body/eval_jaxpr/ppermute | solution.py:15
  55.8 5.7 %collective-permute-start.1 = (bf16[768]{0:T(1024)(128)(2,1)S(1)}, bf16[768]{0:T(1024)(128)(2,1)S(1)}, u32[]{:S(2)}, u32[]{:S(2)}) collective-permute-start(bf16[768]{0:T(1024)(128)(2,1)S(1)} %get-tuple-element.179), channel_id=1, source_target_pairs={{0,15},{1,0},{2,1},{3,2},{4,3},{5,4},{6,5},{7,6},{8,7},{9,8},{10,9... | collective-permute-start | bytes 4616 | tf_op jit(solution)/shard_map/while/body/eval_jaxpr/ppermute | solution.py:15
  60.3 5.7 %collective-permute-start.3 = (bf16[768]{0:T(1024)(128)(2,1)S(1)}, bf16[768]{0:T(1024)(128)(2,1)S(1)}, u32[]{:S(2)}, u32[]{:S(2)}) collective-permute-start(bf16[768]{0:T(1024)(128)(2,1)S(1)} %get-tuple-element.177), channel_id=1, source_target_pairs={{0,1},{1,2},{2,3},{3,4},{4,5},{5,6},{6,7},{7,8},{8,9},{9,10},{10,1... | collective-permute-start | bytes 4616 | tf_op jit(solution)/shard_map/while/body/eval_jaxpr/ppermute | solution.py:15
  70.5 10.3 %collective-permute-start = (bf16[768,256]{1,0:T(8,128)(2,1)S(1)}, bf16[768,256]{1,0:T(8,128)(2,1)S(1)}, u32[]{:S(2)}, u32[]{:S(2)}) collective-permute-start(bf16[768,256]{1,0:T(8,128)(2,1)S(1)} %get-tuple-element.178), channel_id=1, source_target_pairs={{0,15},{1,0},{2,1},{3,2},{4,3},{5,4},{6,5},{7,6},{8,7},{9,8},{10,9... | collective-permute-start | bytes 1179656 | tf_op jit(solution)/shard_map/while/body/eval_jaxpr/ppermute | solution.py:15
  70.6 10.4 %collective-permute-start.2 = (bf16[768,256]{1,0:T(8,128)(2,1)S(1)}, bf16[768,256]{1,0:T(8,128)(2,1)S(1)}, u32[]{:S(2)}, u32[]{:S(2)}) collective-permute-start(bf16[768,256]{1,0:T(8,128)(2,1)S(1)} %get-tuple-element.176), channel_id=1, source_target_pairs={{0,1},{1,2},{2,3},{3,4},{4,5},{5,6},{6,7},{7,8},{8,9},{9,10},{10,1... | collective-permute-start | bytes 1179656 | tf_op jit(solution)/shard_map/while/body/eval_jaxpr/ppermute | solution.py:15
  71.1 5.3 %collective-permute-start.1 = (bf16[768]{0:T(1024)(128)(2,1)S(1)}, bf16[768]{0:T(1024)(128)(2,1)S(1)}, u32[]{:S(2)}, u32[]{:S(2)}) collective-permute-start(bf16[768]{0:T(1024)(128)(2,1)S(1)} %get-tuple-element.179), channel_id=1, source_target_pairs={{0,15},{1,0},{2,1},{3,2},{4,3},{5,4},{6,5},{7,6},{8,7},{9,8},{10,9... | collective-permute-start | bytes 4616 | tf_op jit(solution)/shard_map/while/body/eval_jaxpr/ppermute | solution.py:15
  75.1 5.7 %collective-permute-start.3 = (bf16[768]{0:T(1024)(128)(2,1)S(1)}, bf16[768]{0:T(1024)(128)(2,1)S(1)}, u32[]{:S(2)}, u32[]{:S(2)}) collective-permute-start(bf16[768]{0:T(1024)(128)(2,1)S(1)} %get-tuple-element.177), channel_id=1, source_target_pairs={{0,1},{1,2},{2,3},{3,4},{4,5},{5,6},{6,7},{7,8},{8,9},{9,10},{10,1... | collective-permute-start | bytes 4616 | tf_op jit(solution)/shard_map/while/body/eval_jaxpr/ppermute | solution.py:15
  85.3 10.3 %collective-permute-start = (bf16[768,256]{1,0:T(8,128)(2,1)S(1)}, bf16[768,256]{1,0:T(8,128)(2,1)S(1)}, u32[]{:S(2)}, u32[]{:S(2)}) collective-permute-start(bf16[768,256]{1,0:T(8,128)(2,1)S(1)} %get-tuple-element.178), channel_id=1, source_target_pairs={{0,15},{1,0},{2,1},{3,2},{4,3},{5,4},{6,5},{7,6},{8,7},{9,8},{10,9... | collective-permute-start | bytes 1179656 | tf_op jit(solution)/shard_map/while/body/eval_jaxpr/ppermute | solution.py:15
  85.4 10.4 %collective-permute-start.2 = (bf16[768,256]{1,0:T(8,128)(2,1)S(1)}, bf16[768,256]{1,0:T(8,128)(2,1)S(1)}, u32[]{:S(2)}, u32[]{:S(2)}) collective-permute-start(bf16[768,256]{1,0:T(8,128)(2,1)S(1)} %get-tuple-element.176), channel_id=1, source_target_pairs={{0,1},{1,2},{2,3},{3,4},{4,5},{5,6},{6,7},{7,8},{8,9},{9,10},{10,1... | collective-permute-start | bytes 1179656 | tf_op jit(solution)/shard_map/while/body/eval_jaxpr/ppermute | solution.py:15
  86.9 4.3 %collective-permute-start.1 = (bf16[768]{0:T(1024)(128)(2,1)S(1)}, bf16[768]{0:T(1024)(128)(2,1)S(1)}, u32[]{:S(2)}, u32[]{:S(2)}) collective-permute-start(bf16[768]{0:T(1024)(128)(2,1)S(1)} %get-tuple-element.179), channel_id=1, source_target_pairs={{0,15},{1,0},{2,1},{3,2},{4,3},{5,4},{6,5},{7,6},{8,7},{9,8},{10,9... | collective-permute-start | bytes 4616 | tf_op jit(solution)/shard_map/while/body/eval_jaxpr/ppermute | solution.py:15
  89.9 5.7 %collective-permute-start.3 = (bf16[768]{0:T(1024)(128)(2,1)S(1)}, bf16[768]{0:T(1024)(128)(2,1)S(1)}, u32[]{:S(2)}, u32[]{:S(2)}) collective-permute-start(bf16[768]{0:T(1024)(128)(2,1)S(1)} %get-tuple-element.177), channel_id=1, source_target_pairs={{0,1},{1,2},{2,3},{3,4},{4,5},{5,6},{6,7},{7,8},{8,9},{9,10},{10,1... | collective-permute-start | bytes 4616 | tf_op jit(solution)/shard_map/while/body/eval_jaxpr/ppermute | solution.py:15
  100.2 0.9 copy-start.2
  135.9 34.5 %copy-start = (f32[768,256]{1,0:T(8,128)S(1)}, f32[768,256]{1,0:T(8,128)}, u32[]{:S(2)}) copy-start(f32[768,256]{1,0:T(8,128)} %all-reduce.3.cloned.1.call-done) | copy-start | bytes 2359300
Sparse Core Ops, SparseCore 0:
  101.2 34.6 all-reduce.2
where the time goes:
time: 179 us; the launch traced here: 178 us
  waiting for transfers between devices  72.6 us (41%)
  starting transfers between devices  38.7 us (22%)
  blocking collectives  33 us (18%)
  matrix products  14.1 us (8%)
  between operations  13.5 us (8%)
  other arithmetic  5.07 us (3%)
    ppermute x18, starting transfers between devices, from_behind(): lax.ppermute(x, axis, [(i, (i + by) % devices) for i in range(devices)])  38.7 us
    ppermute x18, waiting for transfers between devices, from_behind(): lax.ppermute(x, axis, [(i, (i + by) % devices) for i in range(devices)])  37.7 us
    psum x1, waiting for transfers between devices, shards(): row_sums = lax.psum(partial_value, 'layer')  34.8 us
    psum x1, blocking collectives, shards(): lax.psum((jnp.sum(member_f * row_sums, axis=0), jnp.sum(member_f, axis=0)...  33 us
    dot_general x8, matrix products, accumulate(): jnp.dot(kernel, onehot, preferred_element_type=jnp.float32)  14.1 us
  transfers between devices with their start and end apart: 19, of which 9 were waited for; matrix products, arithmetic and copies ran while one was open for 1% of the time, Pallas kernels for 0%

commit v1 on v0

--- a/solution.py
+++ b/solution.py
@@ -4,6 +4,11 @@
 from jax.sharding import PartitionSpec as P
 
 K = 256
+
+
+def summed_here(array, name):
+    shards = lax.all_gather(array, name)
+    return jnp.sum(shards, axis=0)
 
 
 def as_sent(x):
@@ -84,7 +89,7 @@
         split_turn,
         (partial_value, climbing[0], climbing[1], falling[0], falling[1]),
     )[0]
-    row_sums = lax.psum(partial_value, "layer")
+    row_sums = summed_here(partial_value, "layer")
     member_f = (labels[:, None] == jnp.arange(K, dtype=jnp.int32)[None, :]).astype(jnp.float32)
     within, counts = lax.psum(
         (jnp.sum(member_f * row_sums, axis=0), jnp.sum(member_f, axis=0)), "blk"

time: 179 us -> 172 us (0.961)
  waiting for transfers between devices: 72.6 us -> 63.7 us
  other arithmetic: 5.07 us -> 7.86 us
    psum x1 -> x0, waiting for transfers between devices: 34.8 us -> none  [shards(): row_sums = lax.psum(partial_value, 'layer')]
    all_gather x0 -> x1, waiting for transfers between devices: none -> 27.6 us  [summed_here(): shards = lax.all_gather(array, name)]
  transfers between devices with their start and end apart: 19 -> 19, of which waited for: 9 -> 9; matrix products, arithmetic and copies ran while one was open for 1% -> 2% of each run, Pallas kernels for 0% -> 0%
where the time goes in v1:
time: 172 us; the launch traced here: 171 us
  waiting for transfers between devices  63.7 us (37%)
  starting transfers between devices  38 us (22%)
  blocking collectives  33 us (19%)
  matrix products  14.1 us (8%)
  between operations  13.5 us (8%)
  other arithmetic  7.86 us (5%)
    ppermute x18, starting transfers between devices, from_behind(): lax.ppermute(x, axis, [(i, (i + by) % devices) for i in range(devices)])  38 us
    ppermute x18, waiting for transfers between devices, from_behind(): lax.ppermute(x, axis, [(i, (i + by) % devices) for i in range(devices)])  36.1 us
    psum x1, blocking collectives, shards(): lax.psum((jnp.sum(member_f * row_sums, axis=0), jnp.sum(member_f, axis=0)...  33 us
    all_gather x1, waiting for transfers between devices, summed_here(): shards = lax.all_gather(array, name)  27.6 us
    dot_general x8, matrix products, accumulate(): jnp.dot(kernel, onehot, preferred_element_type=jnp.float32)  14.1 us
  transfers between devices with their start and end apart: 19, of which 9 were waited for; matrix products, arithmetic and copies ran while one was open for 2% of the time, Pallas kernels for 0%

profile of v1, /device:TPU:0, one launch (start us, length us, event | category | flops | bytes accessed | tf_op | source)
XLA Modules:
  0.0 171.4 jit_solution(13927080865881720366)
XLA Ops:
  6.5 4.1 %collective-permute-start.4 = (bf16[768,256]{1,0:T(8,128)(2,1)}, bf16[768,256]{1,0:T(8,128)(2,1)S(1)}, u32[]{:S(2)}, u32[]{:S(2)}) collective-permute-start(bf16[768,256]{1,0:T(8,128)(2,1)} %param.4), channel_id=1, source_target_pairs={{0,8},{1,9},{2,10},{3,11},{4,12},{5,13},{6,14},{7,15},{8,0},{9,1},... | collective-permute-start | bytes 1179656 | tf_op jit(solution)/shard_map/ppermute | solution.py:20
  10.6 17.8 %collective-permute-done.4 = bf16[768,256]{1,0:T(8,128)(2,1)S(1)} collective-permute-done((bf16[768,256]{1,0:T(8,128)(2,1)}, bf16[768,256]{1,0:T(8,128)(2,1)S(1)}, u32[]{:S(2)}, u32[]{:S(2)}) %collective-permute-start.4) | collective-permute-done | bytes 393248 | tf_op jit(solution)/shard_map/ppermute | solution.py:20
  30.3 5.0 %collective-permute-start.5 = (bf16[768,256]{1,0:T(8,128)(2,1)S(1)}, bf16[768,256]{1,0:T(8,128)(2,1)S(1)}, u32[]{:S(2)}, u32[]{:S(2)}) collective-permute-start(bf16[768,256]{1,0:T(8,128)(2,1)S(1)} %broadcast_select_fusion), channel_id=1, source_target_pairs={{0,4},{1,5},{2,6},{3,7},{4,8},{5,9},{6,10},{7,11},{8,12},{9,13},{1... | collective-permute-start | bytes 1179656 | tf_op jit(solution)/shard_map/ppermute | solution.py:20
  36.1 5.0 %collective-permute-start.9 = (bf16[768]{0:T(1024)(128)(2,1)S(1)}, bf16[768]{0:T(1024)(128)(2,1)S(1)}, u32[]{:S(2)}, u32[]{:S(2)}) collective-permute-start(bf16[768]{0:T(1024)(128)(2,1)S(1)} %broadcast_select_fusion.1), channel_id=1, source_target_pairs={{0,3},{1,4},{2,5},{3,6},{4,7},{5,8},{6,9},{7,10},{8,11},{9,12},{10... | collective-permute-start | bytes 4616 | tf_op jit(solution)/shard_map/ppermute | solution.py:20
  41.0 3.7 %collective-permute-start.7 = (bf16[768]{0:T(1024)(128)(2,1)S(1)}, bf16[768]{0:T(1024)(128)(2,1)S(1)}, u32[]{:S(2)}, u32[]{:S(2)}) collective-permute-start(bf16[768]{0:T(1024)(128)(2,1)S(1)} %broadcast_select_fusion.1), channel_id=1, source_target_pairs={{0,4},{1,5},{2,6},{3,7},{4,8},{5,9},{6,10},{7,11},{8,12},{9,13},{1... | collective-permute-start | bytes 4616 | tf_op jit(solution)/shard_map/ppermute | solution.py:20
  49.4 50.8 %while.20 = (s32[]{:T(128)}, f32[768,256]{1,0:T(8,128)S(1)}, bf16[768,256]{1,0:T(8,128)(2,1)S(1)}, bf16[768]{0:T(1024)(128)(2,1)S(1)}, bf16[768,256]{1,0:T(8,128...) while((s32[]{:T(128)}, f32[768,256]{1,0:T(8,128)S(1)}, ...), condition=%wide.region_6.7_spmd.clone.clone, body=%wide.region_3.6_spmd.clone.clone.sunk | while | flops 1217003520 | bytes 10276093 | solution.py:86
  49.4 6.5 %collective-permute-start = (bf16[768,256]{1,0:T(8,128)(2,1)S(1)}, bf16[768,256]{1,0:T(8,128)(2,1)S(1)}, u32[]{:S(2)}, u32[]{:S(2)}) collective-permute-start(bf16[768,256]{1,0:T(8,128)(2,1)S(1)} %get-tuple-element.178), channel_id=1, source_target_pairs={{0,15},{1,0},{2,1},{3,2},{4,3},{5,4},{6,5},{7,6},{8,7},{9,8},{10,9... | collective-permute-start | bytes 1179656 | tf_op jit(solution)/shard_map/while/body/eval_jaxpr/ppermute | solution.py:20
  55.8 4.4 %collective-permute-start.1 = (bf16[768]{0:T(1024)(128)(2,1)S(1)}, bf16[768]{0:T(1024)(128)(2,1)S(1)}, u32[]{:S(2)}, u32[]{:S(2)}) collective-permute-start(bf16[768]{0:T(1024)(128)(2,1)S(1)} %get-tuple-element.179), channel_id=1, source_target_pairs={{0,15},{1,0},{2,1},{3,2},{4,3},{5,4},{6,5},{7,6},{8,7},{9,8},{10,9... | collective-permute-start | bytes 4616 | tf_op jit(solution)/shard_map/while/body/eval_jaxpr/ppermute | solution.py:20
  61.6 4.4 %collective-permute-done.3 = bf16[768]{0:T(1024)(128)(2,1)S(1)} collective-permute-done((bf16[768]{0:T(1024)(128)(2,1)S(1)}, bf16[768]{0:T(1024)(128)(2,1)S(1)}, u32[]{:S(2)}, u32[]{:S(2)}) %collective-permute-start.3) | collective-permute-done | bytes 1568 | tf_op jit(solution)/shard_map/while/body/eval_jaxpr/ppermute | solution.py:20
  66.4 1.8 %fusion.63 = f32[768,256]{1,0:T(8,128)} fusion(bf16[768,256]{1,0:T(8,128)(2,1)S(1)} %get-tuple-element.190, bf16[768,256]{1,0:T(8,128)(2,1)S(1)} %collective-permute-done, f32[768]{0:T(1024)S(1)} %multiply_reduce_fusion.7, f32[768]{0:T(1024)S(1)} %get-tuple-element.189, f32[768]{0:T(1024)S(1)} %convert_element_type.105), kind=kOutput, calls=%fused_computation.4.clone.1 | convolution fusion | flops 607715328 | bytes 1582080 | tf_op jit(solution)/shard_map/while/body/eval_jaxpr/dot_general | solution.py:53
  68.3 2.2 %fusion.64 = f32[768,256]{1,0:T(8,128)S(1)} fusion(f32[768,256]{1,0:T(8,128)} %fusion.63, f32[768,256]{1,0:T(8,128)S(1)} %get-tuple-element.175, bf16[768,256]{1,0:T(8,128)(2,1)S(1)} %get-tuple-element.190, bf16[768,256]{1,0:T(8,128)(2,1)S(1)} %collective-permute-done.2, f32[768]{0:T(1024)S(1)} %multiply_reduce_fusion.8, ...), kind=kOutput, calls=%fused_computation.6.clone.1 | convolution fusion | flops 608108544 | bytes 3154944 | tf_op jit(solution)/shard_map/while/body/eval_jaxpr/dot_general | solution.py:53
  71.1 4.0 %collective-permute-start.1 = (bf16[768]{0:T(1024)(128)(2,1)S(1)}, bf16[768]{0:T(1024)(128)(2,1)S(1)}, u32[]{:S(2)}, u32[]{:S(2)}) collective-permute-start(bf16[768]{0:T(1024)(128)(2,1)S(1)} %get-tuple-element.179), channel_id=1, source_target_pairs={{0,15},{1,0},{2,1},{3,2},{4,3},{5,4},{6,5},{7,6},{8,7},{9,8},{10,9... | collective-permute-start | bytes 4616 | tf_op jit(solution)/shard_map/while/body/eval_jaxpr/ppermute | solution.py:20
  76.4 4.4 %collective-permute-done.3 = bf16[768]{0:T(1024)(128)(2,1)S(1)} collective-permute-done((bf16[768]{0:T(1024)(128)(2,1)S(1)}, bf16[768]{0:T(1024)(128)(2,1)S(1)}, u32[]{:S(2)}, u32[]{:S(2)}) %collective-permute-start.3) | collective-permute-done | bytes 1568 | tf_op jit(solution)/shard_map/while/body/eval_jaxpr/ppermute | solution.py:20
  81.3 1.8 %fusion.63 = f32[768,256]{1,0:T(8,128)} fusion(bf16[768,256]{1,0:T(8,128)(2,1)S(1)} %get-tuple-element.190, bf16[768,256]{1,0:T(8,128)(2,1)S(1)} %collective-permute-done, f32[768]{0:T(1024)S(1)} %multiply_reduce_fusion.7, f32[768]{0:T(1024)S(1)} %get-tuple-element.189, f32[768]{0:T(1024)S(1)} %convert_element_type.105), kind=kOutput, calls=%fused_computation.4.clone.1 | convolution fusion | flops 607715328 | bytes 1582080 | tf_op jit(solution)/shard_map/while/body/eval_jaxpr/dot_general | solution.py:53
  83.1 2.2 %fusion.64 = f32[768,256]{1,0:T(8,128)S(1)} fusion(f32[768,256]{1,0:T(8,128)} %fusion.63, f32[768,256]{1,0:T(8,128)S(1)} %get-tuple-element.175, bf16[768,256]{1,0:T(8,128)(2,1)S(1)} %get-tuple-element.190, bf16[768,256]{1,0:T(8,128)(2,1)S(1)} %collective-permute-done.2, f32[768]{0:T(1024)S(1)} %multiply_reduce_fusion.8, ...), kind=kOutput, calls=%fused_computation.6.clone.1 | convolution fusion | flops 608108544 | bytes 3154944 | tf_op jit(solution)/shard_map/while/body/eval_jaxpr/dot_general | solution.py:53
  85.4 1.4 collective-permute-start.2
  86.9 3.0 %collective-permute-start.1 = (bf16[768]{0:T(1024)(128)(2,1)S(1)}, bf16[768]{0:T(1024)(128)(2,1)S(1)}, u32[]{:S(2)}, u32[]{:S(2)}) collective-permute-start(bf16[768]{0:T(1024)(128)(2,1)S(1)} %get-tuple-element.179), channel_id=1, source_target_pairs={{0,15},{1,0},{2,1},{3,2},{4,3},{5,4},{6,5},{7,6},{8,7},{9,8},{10,9... | collective-permute-start | bytes 4616 | tf_op jit(solution)/shard_map/while/body/eval_jaxpr/ppermute | solution.py:20
  89.9 1.3 collective-permute-done.1
  91.2 4.4 %collective-permute-done.3 = bf16[768]{0:T(1024)(128)(2,1)S(1)} collective-permute-done((bf16[768]{0:T(1024)(128)(2,1)S(1)}, bf16[768]{0:T(1024)(128)(2,1)S(1)}, u32[]{:S(2)}, u32[]{:S(2)}) %collective-permute-start.3) | collective-permute-done | bytes 1568 | tf_op jit(solution)/shard_map/while/body/eval_jaxpr/ppermute | solution.py:20
  96.1 1.8 %fusion.63 = f32[768,256]{1,0:T(8,128)} fusion(bf16[768,256]{1,0:T(8,128)(2,1)S(1)} %get-tuple-element.190, bf16[768,256]{1,0:T(8,128)(2,1)S(1)} %collective-permute-done, f32[768]{0:T(1024)S(1)} %multiply_reduce_fusion.7, f32[768]{0:T(1024)S(1)} %get-tuple-element.189, f32[768]{0:T(1024)S(1)} %convert_element_type.105), kind=kOutput, calls=%fused_computation.4.clone.1 | convolution fusion | flops 607715328 | bytes 1582080 | tf_op jit(solution)/shard_map/while/body/eval_jaxpr/dot_general | solution.py:53
  97.9 2.2 %fusion.64 = f32[768,256]{1,0:T(8,128)S(1)} fusion(f32[768,256]{1,0:T(8,128)} %fusion.63, f32[768,256]{1,0:T(8,128)S(1)} %get-tuple-element.175, bf16[768,256]{1,0:T(8,128)(2,1)S(1)} %get-tuple-element.190, bf16[768,256]{1,0:T(8,128)(2,1)S(1)} %collective-permute-done.2, f32[768]{0:T(1024)S(1)} %multiply_reduce_fusion.8, ...), kind=kOutput, calls=%fused_computation.6.clone.1 | convolution fusion | flops 608108544 | bytes 3154944 | tf_op jit(solution)/shard_map/while/body/eval_jaxpr/dot_general | solution.py:53
  101.1 27.6 %all-gather.3.cloned.1.call-done = f32[1536,256]{1,0:T(8,128)} async-done(((f32[768,256]{1,0:T(8,128)}), f32[1536,256]{1,0:T(8,128)}) %all-gather.3.cloned.1.call-update) | async-done | bytes 1572880 | tf_op jit(solution)/shard_map/all_gather | solution.py:10
  128.7 1.6 reduce_sum.75
  130.5 33.0 %all-reduce = (f32[256]{0:T(256)S(1)}, f32[256]{0:T(256)S(1)}) all-reduce(f32[256]{0:T(256)S(1)} %get-tuple-element.97, f32[256]{0:T(256)S(1)} %get-tuple-element.96), channel_id=1, replica_groups=mesh['layer'=2,'blk'=16] {'blk'}, use_global_device_ids=true, to_apply=%region_11.12 | all-reduce | flops 512 | bytes 4096 | tf_op jit(solution)/shard_map/psum | solution.py:94
  (67 shorter events, 13.8 us)
Async XLA Ops:
  6.5 40.9 %copy-start = (bf16[768,256]{1,0:T(8,128)(2,1)S(1)}, bf16[768,256]{1,0:T(8,128)(2,1)}, u32[]{:S(2)}) copy-start(bf16[768,256]{1,0:T(8,128)(2,1)} %param.4) | copy-start | bytes 1179652
  6.5 122.2 %all-gather.3.cloned.1.call-start = ((), (), s32[]{:S(2)}) async-start(), calls=%async_computation | async-start | bytes 2359296 | tf_op jit(solution)/shard_map/all_gather | solution.py:10
  6.5 21.9 %collective-permute-start.4 = (bf16[768,256]{1,0:T(8,128)(2,1)}, bf16[768,256]{1,0:T(8,128)(2,1)S(1)}, u32[]{:S(2)}, u32[]{:S(2)}) collective-permute-start(bf16[768,256]{1,0:T(8,128)(2,1)} %param.4), channel_id=1, source_target_pairs={{0,8},{1,9},{2,10},{3,11},{4,12},{5,13},{6,14},{7,15},{8,0},{9,1},... | collective-permute-start | bytes 1179656 | tf_op jit(solution)/shard_map/ppermute | solution.py:20
  29.5 17.6 %collective-permute-start.8 = (bf16[768,256]{1,0:T(8,128)(2,1)S(1)}, bf16[768,256]{1,0:T(8,128)(2,1)S(1)}, u32[]{:S(2)}, u32[]{:S(2)}) collective-permute-start(bf16[768,256]{1,0:T(8,128)(2,1)S(1)} %broadcast_select_fusion), channel_id=1, source_target_pairs={{0,3},{1,4},{2,5},{3,6},{4,7},{5,8},{6,9},{7,10},{8,11},{9,12},{10... | collective-permute-start | bytes 1179656 | tf_op jit(solution)/shard_map/ppermute | solution.py:20
  30.3 5.1 %collective-permute-start.6 = (bf16[768]{0:T(1024)(128)(2,1)S(1)}, bf16[768]{0:T(1024)(128)(2,1)S(1)}, u32[]{:S(2)}, u32[]{:S(2)}) collective-permute-start(bf16[768]{0:T(1024)(128)(2,1)S(1)} %convert_element_type.52), channel_id=1, source_target_pairs={{0,8},{1,9},{2,10},{3,11},{4,12},{5,13},{6,14},{7,15},{8,0},{9,1},... | collective-permute-start | bytes 4616 | tf_op jit(solution)/shard_map/ppermute | solution.py:20
  30.3 16.9 %collective-permute-start.5 = (bf16[768,256]{1,0:T(8,128)(2,1)S(1)}, bf16[768,256]{1,0:T(8,128)(2,1)S(1)}, u32[]{:S(2)}, u32[]{:S(2)}) collective-permute-start(bf16[768,256]{1,0:T(8,128)(2,1)S(1)} %broadcast_select_fusion), channel_id=1, source_target_pairs={{0,4},{1,5},{2,6},{3,7},{4,8},{5,9},{6,10},{7,11},{8,12},{9,13},{1... | collective-permute-start | bytes 1179656 | tf_op jit(solution)/shard_map/ppermute | solution.py:20
  36.1 11.0 %collective-permute-start.9 = (bf16[768]{0:T(1024)(128)(2,1)S(1)}, bf16[768]{0:T(1024)(128)(2,1)S(1)}, u32[]{:S(2)}, u32[]{:S(2)}) collective-permute-start(bf16[768]{0:T(1024)(128)(2,1)S(1)} %broadcast_select_fusion.1), channel_id=1, source_target_pairs={{0,3},{1,4},{2,5},{3,6},{4,7},{5,8},{6,9},{7,10},{8,11},{9,12},{10... | collective-permute-start | bytes 4616 | tf_op jit(solution)/shard_map/ppermute | solution.py:20
  41.0 6.0 %collective-permute-start.7 = (bf16[768]{0:T(1024)(128)(2,1)S(1)}, bf16[768]{0:T(1024)(128)(2,1)S(1)}, u32[]{:S(2)}, u32[]{:S(2)}) collective-permute-start(bf16[768]{0:T(1024)(128)(2,1)S(1)} %broadcast_select_fusion.1), channel_id=1, source_target_pairs={{0,4},{1,5},{2,6},{3,7},{4,8},{5,9},{6,10},{7,11},{8,12},{9,13},{1... | collective-permute-start | bytes 4616 | tf_op jit(solution)/shard_map/ppermute | solution.py:20
  49.4 16.6 %collective-permute-start = (bf16[768,256]{1,0:T(8,128)(2,1)S(1)}, bf16[768,256]{1,0:T(8,128)(2,1)S(1)}, u32[]{:S(2)}, u32[]{:S(2)}) collective-permute-start(bf16[768,256]{1,0:T(8,128)(2,1)S(1)} %get-tuple-element.178), channel_id=1, source_target_pairs={{0,15},{1,0},{2,1},{3,2},{4,3},{5,4},{6,5},{7,6},{8,7},{9,8},{10,9... | collective-permute-start | bytes 1179656 | tf_op jit(solution)/shard_map/while/body/eval_jaxpr/ppermute | solution.py:20
  55.8 10.4 %collective-permute-start.2 = (bf16[768,256]{1,0:T(8,128)(2,1)S(1)}, bf16[768,256]{1,0:T(8,128)(2,1)S(1)}, u32[]{:S(2)}, u32[]{:S(2)}) collective-permute-start(bf16[768,256]{1,0:T(8,128)(2,1)S(1)} %get-tuple-element.176), channel_id=1, source_target_pairs={{0,1},{1,2},{2,3},{3,4},{4,5},{5,6},{6,7},{7,8},{8,9},{9,10},{10,1... | collective-permute-start | bytes 1179656 | tf_op jit(solution)/shard_map/while/body/eval_jaxpr/ppermute | solution.py:20
  55.8 5.7 %collective-permute-start.1 = (bf16[768]{0:T(1024)(128)(2,1)S(1)}, bf16[768]{0:T(1024)(128)(2,1)S(1)}, u32[]{:S(2)}, u32[]{:S(2)}) collective-permute-start(bf16[768]{0:T(1024)(128)(2,1)S(1)} %get-tuple-element.179), channel_id=1, source_target_pairs={{0,15},{1,0},{2,1},{3,2},{4,3},{5,4},{6,5},{7,6},{8,7},{9,8},{10,9... | collective-permute-start | bytes 4616 | tf_op jit(solution)/shard_map/while/body/eval_jaxpr/ppermute | solution.py:20
  60.3 5.7 %collective-permute-start.3 = (bf16[768]{0:T(1024)(128)(2,1)S(1)}, bf16[768]{0:T(1024)(128)(2,1)S(1)}, u32[]{:S(2)}, u32[]{:S(2)}) collective-permute-start(bf16[768]{0:T(1024)(128)(2,1)S(1)} %get-tuple-element.177), channel_id=1, source_target_pairs={{0,1},{1,2},{2,3},{3,4},{4,5},{5,6},{6,7},{7,8},{8,9},{9,10},{10,1... | collective-permute-start | bytes 4616 | tf_op jit(solution)/shard_map/while/body/eval_jaxpr/ppermute | solution.py:20
  70.5 10.3 %collective-permute-start = (bf16[768,256]{1,0:T(8,128)(2,1)S(1)}, bf16[768,256]{1,0:T(8,128)(2,1)S(1)}, u32[]{:S(2)}, u32[]{:S(2)}) collective-permute-start(bf16[768,256]{1,0:T(8,128)(2,1)S(1)} %get-tuple-element.178), channel_id=1, source_target_pairs={{0,15},{1,0},{2,1},{3,2},{4,3},{5,4},{6,5},{7,6},{8,7},{9,8},{10,9... | collective-permute-start | bytes 1179656 | tf_op jit(solution)/shard_map/while/body/eval_jaxpr/ppermute | solution.py:20
  70.6 10.4 %collective-permute-start.2 = (bf16[768,256]{1,0:T(8,128)(2,1)S(1)}, bf16[768,256]{1,0:T(8,128)(2,1)S(1)}, u32[]{:S(2)}, u32[]{:S(2)}) collective-permute-start(bf16[768,256]{1,0:T(8,128)(2,1)S(1)} %get-tuple-element.176), channel_id=1, source_target_pairs={{0,1},{1,2},{2,3},{3,4},{4,5},{5,6},{6,7},{7,8},{8,9},{9,10},{10,1... | collective-permute-start | bytes 1179656 | tf_op jit(solution)/shard_map/while/body/eval_jaxpr/ppermute | solution.py:20
  71.1 5.3 %collective-permute-start.1 = (bf16[768]{0:T(1024)(128)(2,1)S(1)}, bf16[768]{0:T(1024)(128)(2,1)S(1)}, u32[]{:S(2)}, u32[]{:S(2)}) collective-permute-start(bf16[768]{0:T(1024)(128)(2,1)S(1)} %get-tuple-element.179), channel_id=1, source_target_pairs={{0,15},{1,0},{2,1},{3,2},{4,3},{5,4},{6,5},{7,6},{8,7},{9,8},{10,9... | collective-permute-start | bytes 4616 | tf_op jit(solution)/shard_map/while/body/eval_jaxpr/ppermute | solution.py:20
  75.1 5.7 %collective-permute-start.3 = (bf16[768]{0:T(1024)(128)(2,1)S(1)}, bf16[768]{0:T(1024)(128)(2,1)S(1)}, u32[]{:S(2)}, u32[]{:S(2)}) collective-permute-start(bf16[768]{0:T(1024)(128)(2,1)S(1)} %get-tuple-element.177), channel_id=1, source_target_pairs={{0,1},{1,2},{2,3},{3,4},{4,5},{5,6},{6,7},{7,8},{8,9},{9,10},{10,1... | collective-permute-start | bytes 4616 | tf_op jit(solution)/shard_map/while/body/eval_jaxpr/ppermute | solution.py:20
  85.3 10.3 %collective-permute-start = (bf16[768,256]{1,0:T(8,128)(2,1)S(1)}, bf16[768,256]{1,0:T(8,128)(2,1)S(1)}, u32[]{:S(2)}, u32[]{:S(2)}) collective-permute-start(bf16[768,256]{1,0:T(8,128)(2,1)S(1)} %get-tuple-element.178), channel_id=1, source_target_pairs={{0,15},{1,0},{2,1},{3,2},{4,3},{5,4},{6,5},{7,6},{8,7},{9,8},{10,9... | collective-permute-start | bytes 1179656 | tf_op jit(solution)/shard_map/while/body/eval_jaxpr/ppermute | solution.py:20
  85.4 10.4 %collective-permute-start.2 = (bf16[768,256]{1,0:T(8,128)(2,1)S(1)}, bf16[768,256]{1,0:T(8,128)(2,1)S(1)}, u32[]{:S(2)}, u32[]{:S(2)}) collective-permute-start(bf16[768,256]{1,0:T(8,128)(2,1)S(1)} %get-tuple-element.176), channel_id=1, source_target_pairs={{0,1},{1,2},{2,3},{3,4},{4,5},{5,6},{6,7},{7,8},{8,9},{9,10},{10,1... | collective-permute-start | bytes 1179656 | tf_op jit(solution)/shard_map/while/body/eval_jaxpr/ppermute | solution.py:20
  86.9 4.3 %collective-permute-start.1 = (bf16[768]{0:T(1024)(128)(2,1)S(1)}, bf16[768]{0:T(1024)(128)(2,1)S(1)}, u32[]{:S(2)}, u32[]{:S(2)}) collective-permute-start(bf16[768]{0:T(1024)(128)(2,1)S(1)} %get-tuple-element.179), channel_id=1, source_target_pairs={{0,15},{1,0},{2,1},{3,2},{4,3},{5,4},{6,5},{7,6},{8,7},{9,8},{10,9... | collective-permute-start | bytes 4616 | tf_op jit(solution)/shard_map/while/body/eval_jaxpr/ppermute | solution.py:20
  89.9 5.7 %collective-permute-start.3 = (bf16[768]{0:T(1024)(128)(2,1)S(1)}, bf16[768]{0:T(1024)(128)(2,1)S(1)}, u32[]{:S(2)}, u32[]{:S(2)}) collective-permute-start(bf16[768]{0:T(1024)(128)(2,1)S(1)} %get-tuple-element.177), channel_id=1, source_target_pairs={{0,1},{1,2},{2,3},{3,4},{4,5},{5,6},{6,7},{7,8},{8,9},{9,10},{10,1... | collective-permute-start | bytes 4616 | tf_op jit(solution)/shard_map/while/body/eval_jaxpr/ppermute | solution.py:20
  100.1 0.9 copy-start.1
  100.2 30.2 %copy-start.2 = (s32[768]{0:T(1024)S(1)}, s32[768]{0:T(1024)}, u32[]{:S(2)}) copy-start(s32[768]{0:T(1024)} %param.5) | copy-start | bytes 9220
Sparse Core Ops, SparseCore 0:
  101.2 27.4 all-gather.2
